TPU v7x, 32 devices: a whole 2x2x4 slice. The times are simulated.
32 devices in a mesh: seq: 16 (over z, y, x), head: 2 (over core).
Axes of the slice: x: 2, y: 2, z: 4, core: 2. Of those that a mesh axis runs over, the one named last changes fastest.
Arguments:
- query_vectors: bfloat16 [4096, 2560], P(('seq', 'head')), may hold values from -6 to 6
- address_vectors: bfloat16 [4096, 2560], P(('seq', 'head')), may hold values from -0.75 to 0.75
- payload_vectors: bfloat16 [4096, 2560], P(('seq', 'head')), may hold values from -6 to 6
- forget_logarithms: bfloat16 [4096, 2560], P(('seq', 'head')), may hold values from -1.5 to 0
- pre_sigmoid_filter: bfloat16 [4096, 2560], P(('seq', 'head')), may hold values from -6 to 6
- current_reward_table: float32 [40, 64], replicated, may hold values from -0.5 to 1.5
- cluster_standardize_weight: float32 [2560], replicated, may hold values from 0.25 to 1.75
- cluster_standardize_offset: float32 [2560], replicated, may hold values from -1.5 to 1.5
Outputs:
- mixed: bfloat16 [4096, 2560], P('seq', 'head')
All inputs are finite; a program needn't handle non-finite values.
Results may differ from a plain program's by a relative error of at most 0.001.
Values may be sent and summed in bfloat16 or wider, within the bound.
No kernel may reach another device: no remote copies, remote signals or barrier semaphores. Data moves between devices by JAX's collectives and lax.ppermute only.
A program may use at most 192 MiB of HBM per device.

v0:
```python
import math
import jax
import jax.numpy as jnp
from jax import lax
from jax.sharding import PartitionSpec as P

CHANNEL_COUNT = 64


def prefix_2(value, axis, join, neutral):
    count, mine = (lax.axis_size(axis), lax.axis_index(axis))
    pieces = jax.tree.map(lambda part: lax.all_gather(part, axis), value)
    so_far = jax.tree.map(
        lambda part, zero: jnp.full_like(part, 0) + jnp.asarray(zero, part.dtype), value, neutral
    )

    def step(position, so_far):
        longer = join(so_far, jax.tree.map(lambda part: part[position], pieces))
        return jax.tree.map(lambda new, old: jnp.where(position < mine, new, old), longer, so_far)

    return lax.fori_loop(0, count - 1, step, so_far)


def group_heads(array, groups):
    length, hosted_attenders, channels = array.shape
    return array.reshape(length, groups, hosted_attenders // groups, channels).transpose(1, 0, 2, 3)


def block_shares(
    query_vectors, address_vectors, payload_vectors, forget_logarithms, current_reward_piece
):
    length, width = query_vectors.shape
    hosted_attenders = width // CHANNEL_COUNT
    highest = lax.Precision.HIGHEST
    rows = lax.broadcasted_iota(jnp.int32, (length, length), 0)
    columns = lax.broadcasted_iota(jnp.int32, (length, length), 1)
    lower = (rows >= columns).astype(jnp.float32)
    strict = rows > columns
    forget_multiplier = forget_logarithms.astype(jnp.float32)
    cumul = jnp.dot(lower, forget_multiplier, precision=highest)
    before = (cumul - forget_multiplier).reshape(length, hosted_attenders, CHANNEL_COUNT)
    final = cumul[-1].reshape(hosted_attenders, CHANNEL_COUNT)
    cumul = cumul.reshape(length, hosted_attenders, CHANNEL_COUNT)
    incoming_memory = query_vectors.astype(jnp.float32).reshape(
        length, hosted_attenders, CHANNEL_COUNT
    )
    address_block = address_vectors.astype(jnp.float32).reshape(
        length, hosted_attenders, CHANNEL_COUNT
    )
    payload_block = payload_vectors.astype(jnp.float32).reshape(
        length, hosted_attenders, CHANNEL_COUNT
    )
    scaled_receptance = incoming_memory * jnp.exp(before)
    scaled_k = address_block * jnp.exp(-cumul)
    end_keys = address_block * jnp.exp(final[None] - cumul)
    group_size = math.gcd(hosted_attenders, 4)
    groups = hosted_attenders // group_size

    def group_output(pieces):
        receptance_group, keys_group, values_group = pieces
        scores = jnp.einsum("thc,shc->hts", receptance_group, keys_group, precision=highest)
        scores = jnp.where(strict[None], scores, jnp.float32(0.0))
        return jnp.einsum("hts,shj->thj", scores, values_group, precision=highest)

    grouped = lax.map(
        group_output,
        (
            group_heads(scaled_receptance, groups),
            group_heads(scaled_k, groups),
            group_heads(payload_block, groups),
        ),
    )
    within = grouped.transpose(1, 0, 2, 3).reshape(length, hosted_attenders, CHANNEL_COUNT)
    diagonal_piece = jnp.sum(incoming_memory * current_reward_piece[None] * address_block, axis=2)
    mixed_output = within + diagonal_piece[:, :, None] * payload_block
    slab_ends = jnp.einsum("shc,shj->hcj", end_keys, payload_block, precision=highest)
    return (mixed_output, scaled_receptance, jnp.exp(final), slab_ends)


def join_states(earlier, later):
    return (earlier[0] * later[0], later[0][:, :, None] * earlier[1] + later[1])


def finish(mixed_output, scaled_receptance, prefix, pre_sigmoid_filter, gain, bias):
    mixed_output = mixed_output + jnp.einsum(
        "thc,hcj->thj", scaled_receptance, prefix, precision=lax.Precision.HIGHEST
    )
    length = mixed_output.shape[0]
    center = mixed_output - jnp.mean(mixed_output, axis=2, keepdims=True)
    spread = jnp.mean(center * center, axis=2, keepdims=True)
    normed = (center * lax.rsqrt(spread + 1e-05)).reshape(length, -1)
    gate = pre_sigmoid_filter.astype(jnp.float32)
    return ((normed * gain[None] + bias[None]) * gate * jax.nn.sigmoid(gate)).astype(jnp.bfloat16)


def body(
    query_vectors,
    address_vectors,
    payload_vectors,
    forget_logarithms,
    pre_sigmoid_filter,
    current_reward_table,
    cluster_standardize_weight,
    cluster_standardize_offset,
):
    incoming_memory, address_block, payload_block, forget_multiplier, gate = (
        lax.all_to_all(query_vectors, "head", split_axis=1, concat_axis=0, tiled=True),
        lax.all_to_all(address_vectors, "head", split_axis=1, concat_axis=0, tiled=True),
        lax.all_to_all(payload_vectors, "head", split_axis=1, concat_axis=0, tiled=True),
        lax.all_to_all(forget_logarithms, "head", split_axis=1, concat_axis=0, tiled=True),
        lax.all_to_all(pre_sigmoid_filter, "head", split_axis=1, concat_axis=0, tiled=True),
    )
    width = incoming_memory.shape[1]
    hosted_attenders = width // CHANNEL_COUNT
    block_offset = lax.axis_index("head")
    current_reward_piece = lax.dynamic_slice_in_dim(
        current_reward_table, block_offset * hosted_attenders, hosted_attenders, 0
    )
    gain = lax.dynamic_slice_in_dim(cluster_standardize_weight, block_offset * width, width, 0)
    bias = lax.dynamic_slice_in_dim(cluster_standardize_offset, block_offset * width, width, 0)
    mixed_output, scaled_receptance, decay_total, slab_ends = block_shares(
        incoming_memory, address_block, payload_block, forget_multiplier, current_reward_piece
    )
    identity = (jnp.ones_like(decay_total), jnp.zeros_like(slab_ends))
    carried = prefix_2((decay_total, slab_ends), "seq", join_states, identity)
    return finish(mixed_output, scaled_receptance, carried[1], gate, gain, bias)


def solution(mesh):
    return jax.shard_map(
        body,
        mesh=mesh,
        in_specs=(
            P(("seq", "head"), None),
            P(("seq", "head"), None),
            P(("seq", "head"), None),
            P(("seq", "head"), None),
            P(("seq", "head"), None),
            P(),
            P(),
            P(),
        ),
        out_specs=P("seq", "head"),
        check_vma=False,
    )
```

profile of v0, /device:TPU:0, one launch (start us, length us, event | category | flops | bytes accessed | tf_op | source)
XLA Modules:
  0.0 217.2 jit_solution(4822067310482961612)
XLA Ops:
  6.5 2.0 copy.72
  8.6 3.5 %all-to-all-start.2 = ((bf16[128,2,1280]{2,0,1:T(8,128)(2,1)}), bf16[128,2,1280]{2,0,1:T(8,128)(2,1)S(1)}, u32[]{:S(2)}, u32[]{:S(2)}) async-start(bf16[128,2,1280]{2,0,1:T(8,128)(2,1)} %bitcast.92), calls=%async_computation.2 | async-start | bytes 1310720 | tf_op jit(solution)/shard_map/all_to_all | solution.py:110
  12.1 1.1 copy.55
  13.2 0.7 all-to-all-done.2
  13.9 3.5 %all-to-all-start.3 = ((bf16[128,2,1280]{0,2,1:T(8,128)(2,1)}), bf16[128,2,1280]{0,2,1:T(8,128)(2,1)S(1)}, u32[]{:S(2)}, u32[]{:S(2)}) async-start(bf16[128,2,1280]{0,2,1:T(8,128)(2,1)} %bitcast.10), calls=%async_computation.3 | async-start | bytes 1310720 | tf_op jit(solution)/shard_map/all_to_all | solution.py:108
  17.4 2.0 negate_exponential_fusion
  19.5 1.5 copy.61
  21.0 1.1 copy.49
  22.0 3.5 %all-to-all-start = ((bf16[128,2,1280]{0,2,1:T(8,128)(2,1)}), bf16[128,2,1280]{0,2,1:T(8,128)(2,1)S(1)}, u32[]{:S(2)}, u32[]{:S(2)}) async-start(bf16[128,2,1280]{0,2,1:T(8,128)(2,1)} %bitcast), calls=%async_computation | async-start | bytes 1310720 | tf_op jit(solution)/shard_map/all_to_all | solution.py:109
  25.7 4.8 %copy.56 = f32[2,128,1280]{1,0,2:T(2,128)S(1)} copy(f32[2,128,1280]{1,2,0:T(8,128)S(1)} %convert_bitcast_fusion) | data formatting | bytes 2621440 | tf_op jit(solution)/shard_map/convert_element_type | solution.py:47
  30.5 1.0 reshape.91
  31.6 0.8 copy-done.4
  32.4 6.1 %copy.60 = bf16[2,128,1280]{1,0,2:T(2,128)(2,1)} copy(bf16[2,128,1280]{1,2,0:T(8,128)(2,1)S(1)} %bitcast.110) | data formatting | bytes 1310720 | tf_op jit(solution)/shard_map/all_to_all | solution.py:109
  38.5 2.2 %all_to_all.69 = bf16[256,20,64]{0,2,1:T(8,128)(2,1)S(1)} reshape(bf16[2,128,1280]{1,0,2:T(2,128)(2,1)} %copy.60) | data formatting | bytes 1310720 | tf_op jit(solution)/shard_map/all_to_all | solution.py:109
  40.8 3.3 %fusion.22 = f32[20,64,64]{2,1,0:T(8,128)} fusion(bf16[256,20,64]{0,2,1:T(8,128)(2,1)S(1)} %all_to_all.69, f32[256,20,64]{0,2,1:T(8,128)S(1)} %reshape.91, f32[256,20,64]{0,2,1:T(8,128)} %bitcast.111, f32[20,64]{1,0:T(8,128)S(1)} %sub.22), kind=kOutput, calls=%fused_computation.32 | convolution fusion | flops 252313600 | bytes 3609600 | tf_op jit(solution)/shard_map/shc,shj->hcj/dot_general | solution.py:76
  44.1 2.2 %copy.51 = bf16[128,2560]{0,1:T(8,128)(2,1)} copy(bf16[128,2560]{1,0:T(8,128)(2,1)} %param.12) | data formatting | bytes 1310720 | tf_op args[0]
  46.3 3.7 %all-to-all-start.1 = ((bf16[128,2,1280]{0,2,1:T(8,128)(2,1)}), bf16[128,2,1280]{0,2,1:T(8,128)(2,1)S(1)}, u32[]{:S(2)}, u32[]{:S(2)}) async-start(bf16[128,2,1280]{0,2,1:T(8,128)(2,1)} %bitcast.3), calls=%async_computation.1 | async-start | bytes 1310720 | tf_op jit(solution)/shard_map/all_to_all | solution.py:107
  50.0 2.1 reshape.89
  52.1 2.0 copy.71
  54.1 4.3 %all-to-all-start.4 = ((bf16[128,2,1280]{2,0,1:T(8,128)(2,1)}), bf16[128,2,1280]{2,0,1:T(8,128)(2,1)}, u32[]{:S(2)}, u32[]{:S(2)}) async-start(bf16[128,2,1280]{2,0,1:T(8,128)(2,1)} %bitcast.91), calls=%async_computation.4 | async-start | bytes 1310720 | tf_op jit(solution)/shard_map/all_to_all | solution.py:111
  58.5 4.8 %copy.52 = f32[2,128,1280]{1,0,2:T(2,128)S(1)} copy(f32[2,128,1280]{1,2,0:T(8,128)S(1)} %convert_bitcast_fusion.1) | data formatting | bytes 2621440 | tf_op jit(solution)/shard_map/convert_element_type | solution.py:44
  63.3 1.1 copy-done.1
  64.3 2.1 reshape.88
  66.5 2.3 %reshape.90 = f32[256,20,64]{0,2,1:T(8,128)S(1)} reshape(f32[2,128,1280]{1,0,2:T(2,128)} %copy-done.1) | data formatting | bytes 2621440 | tf_op jit(solution)/shard_map/convert_element_type | solution.py:44
  68.8 2.8 %copy.54 = f32[256,1280]{0,1:T(8,128)} copy(f32[256,1280]{1,0:T(8,128)} %get-tuple-element.191) | data formatting | bytes 2621440 | tf_op jit(solution)/shard_map/exp | solution.py:53
  71.6 2.8 %copy.57 = f32[256,1280]{0,1:T(8,128)} copy(f32[256,1280]{1,0:T(8,128)} %get-tuple-element.190) | data formatting | bytes 2621440 | tf_op jit(solution)/shard_map/exp | solution.py:54
  74.4 1.2 bitcast_convert_fusion
  75.6 5.6 %copy.50 = f32[2,128,1280]{1,0,2:T(2,128)} copy(f32[2,128,1280]{1,2,0:T(8,128)S(1)} %bitcast_convert_fusion) | data formatting | bytes 2621440 | tf_op jit(solution)/shard_map/transpose | solution.py:26
  81.2 3.1 %reshape.93 = f32[256,5,4,64]{0,3,2,1:T(8,128)} reshape(f32[2,128,1280]{1,0,2:T(2,128)} %copy.50) | data formatting | bytes 2621440 | tf_op jit(solution)/shard_map/transpose | solution.py:26
  84.6 45.8 %all_gather.10 = f32[16,20,64]{2,1,0:T(8,128)S(1)} all-gather(f32[1,20,64]{2,1,0:T(8,128)S(1)} %exp.41), channel_id=1, replica_groups=mesh['seq'=16,'head'=2] {'seq'}, dimensions={0}, use_global_device_ids=true | all-gather | bytes 87040 | tf_op jit(solution)/shard_map/all_gather | solution.py:12
  130.4 3.2 %multiply_bitcast_fusion.1 = f32[5,256,4,64]{1,3,2,0:T(8,128)} fusion(f32[256,5,4,64]{0,3,2,1:T(8,128)} %reshape.88, f32[256,5,4,64]{0,3,2,1:T(8,128)} %bitcast.107), kind=kLoop, calls=%fused_computation.39 | loop fusion | flops 327680 | bytes 3932160 | tf_op jit(solution)/shard_map/transpose | solution.py:26
  133.5 1.2 multiply_bitcast_fusion
  134.8 24.7 %while.25 = (s32[]{:T(128)}, f32[5,256,4,64]{1,3,2,0:T(8,128)}, f32[5,256,4,64]{1,3,2,0:T(8,128)}, f32[5,256,4,64]{1,3,2,0:T(8,128)}, f32[5,256,4,64]{1,3,2,0:T(8,128)}, /*index=5*/s32[]{:T(128)}) while((s32[]{:T(128)}, f32[5,256,4,64]{1,3,2,0:T(8,128)}, f32[5,256,4,64]{1,3,2,0:T(8,128)}, f32[5,256,4,64]{1,3,2,0:T(8,128)}, ...), condition=%wide.region_1.2_spmd.clone, body=%wide.region_0.1_spmd.clone.sunk | while | flops 402980864 | bytes 3278917 | solution.py:65
  134.8 2.1 convolution_select_fusion.2
  136.9 2.8 %fusion.44 = f32[5,256,4,64]{1,3,2,0:T(8,128)} fusion(f32[5,256,4,64]{1,3,2,0:T(8,128)} %get-tuple-element.264, s32[]{:T(128)} %get-tuple-element.263, f32[4,256,256]{2,1,0:T(8,128)S(1)} %convolution_select_fusion.2, f32[5,256,4,64]{1,3,2,0:T(8,128)} %get-tuple-element.271), kind=kOutput, calls=%fused_computation.3.clone.1 | convolution fusion | flops 201326592 | bytes 1573888 | tf_op jit(solution)/shard_map/while/body/eval_jaxpr/hts,shj->thj/dot_general | solution.py:63
  139.7 2.1 convolution_select_fusion.2
  141.8 2.8 %fusion.44 = f32[5,256,4,64]{1,3,2,0:T(8,128)} fusion(f32[5,256,4,64]{1,3,2,0:T(8,128)} %get-tuple-element.264, s32[]{:T(128)} %get-tuple-element.263, f32[4,256,256]{2,1,0:T(8,128)S(1)} %convolution_select_fusion.2, f32[5,256,4,64]{1,3,2,0:T(8,128)} %get-tuple-element.271), kind=kOutput, calls=%fused_computation.3.clone.1 | convolution fusion | flops 201326592 | bytes 1573888 | tf_op jit(solution)/shard_map/while/body/eval_jaxpr/hts,shj->thj/dot_general | solution.py:63
  144.7 2.1 convolution_select_fusion.2
  146.8 2.8 %fusion.44 = f32[5,256,4,64]{1,3,2,0:T(8,128)} fusion(f32[5,256,4,64]{1,3,2,0:T(8,128)} %get-tuple-element.264, s32[]{:T(128)} %get-tuple-element.263, f32[4,256,256]{2,1,0:T(8,128)S(1)} %convolution_select_fusion.2, f32[5,256,4,64]{1,3,2,0:T(8,128)} %get-tuple-element.271), kind=kOutput, calls=%fused_computation.3.clone.1 | convolution fusion | flops 201326592 | bytes 1573888 | tf_op jit(solution)/shard_map/while/body/eval_jaxpr/hts,shj->thj/dot_general | solution.py:63
  149.6 2.1 convolution_select_fusion.2
  151.7 2.8 %fusion.44 = f32[5,256,4,64]{1,3,2,0:T(8,128)} fusion(f32[5,256,4,64]{1,3,2,0:T(8,128)} %get-tuple-element.264, s32[]{:T(128)} %get-tuple-element.263, f32[4,256,256]{2,1,0:T(8,128)S(1)} %convolution_select_fusion.2, f32[5,256,4,64]{1,3,2,0:T(8,128)} %get-tuple-element.271), kind=kOutput, calls=%fused_computation.3.clone.1 | convolution fusion | flops 201326592 | bytes 1573888 | tf_op jit(solution)/shard_map/while/body/eval_jaxpr/hts,shj->thj/dot_general | solution.py:63
  154.5 2.1 convolution_select_fusion.2
  156.6 2.8 %fusion.44 = f32[5,256,4,64]{1,3,2,0:T(8,128)} fusion(f32[5,256,4,64]{1,3,2,0:T(8,128)} %get-tuple-element.264, s32[]{:T(128)} %get-tuple-element.263, f32[4,256,256]{2,1,0:T(8,128)S(1)} %convolution_select_fusion.2, f32[5,256,4,64]{1,3,2,0:T(8,128)} %get-tuple-element.271), kind=kOutput, calls=%fused_computation.3.clone.1 | convolution fusion | flops 201326592 | bytes 1573888 | tf_op jit(solution)/shard_map/while/body/eval_jaxpr/hts,shj->thj/dot_general | solution.py:63
  159.4 3.1 %fusion.15 = f32[256,20,64]{0,2,1:T(8,128)} fusion(f32[256,20,64]{0,2,1:T(8,128)} %bitcast.15, bf16[256,20,64]{0,2,1:T(8,128)(2,1)} %copy-done.3, f32[256,20,64]{0,2,1:T(8,128)S(1)} %reshape.91, f32[256,20,64]{0,2,1:T(8,128)S(1)} %reshape.90, f32[20,64]{1,0:T(8,128)S(1)} %constant_dynamic-slice_fusion), kind=kOutput, calls=%fused_computation.20 | output fusion | flops 1643583 | bytes 5903360 | tf_op jit(solution)/shard_map/mul | solution.py:75
  162.5 18.6 %all-gather.3.cloned.1.call-done = f32[320,64,64]{2,1,0:T(8,128)} async-done(((f32[20,64,64]{2,1,0:T(8,128)}), f32[320,64,64]{2,1,0:T(8,128)}) %all-gather.3.cloned.1.call-update) | async-done | bytes 5242896 | tf_op jit(solution)/shard_map/all_gather | solution.py:12
  181.1 23.3 %while.26 = (s32[]{:T(128)}, f32[20,64,64]{2,1,0:T(8,128)S(1)}, s32[]{:T(128)}, f32[16,20,64]{2,1,0:T(8,128)S(1)}, f32[16,20,64,64]{3,2,1,0:T(8,128)}, /*index=5*/s32[]{:T(128)}, s32[]{:T(128)}) while((s32[]{:T(128)}, f32[20,64,64]{2,1,0:T(8,128)S(1)}, s32[]{:T(128)}, f32[16,20,64]{2,1,0:T(8,128)S(1)}, ...), condition=%wide.region_4.5_spmd.clone, body=%wide.region_3.4_spmd.clone.sunk | while | flops 327684 | bytes 998505 | solution.py:21
  181.1 1.6 fusion.45
  182.8 1.5 fusion.45
  184.3 1.5 fusion.45
  185.9 1.5 fusion.45
  187.4 1.5 fusion.45
  189.0 1.5 fusion.45
  190.5 1.5 fusion.45
  192.1 1.5 fusion.45
  193.6 1.5 fusion.45
  195.2 1.5 fusion.45
  196.7 1.5 fusion.45
  198.3 1.5 fusion.45
  199.8 1.5 fusion.45
  201.4 1.5 fusion.45
  202.9 1.5 fusion.45
  204.5 2.7 %fusion.29 = (f32[256,20]{0,1:T(8,128)S(1)}, f32[256,20,64]{0,2,1:T(8,128)S(1)}) fusion(f32[256,20,64]{0,2,1:T(8,128)} %fusion.15, f32[20,64,64]{2,1,0:T(8,128)S(1)} %get-tuple-element.132, f32[256,20,64]{0,2,1:T(8,128)S(1)} %reshape.90, f32[256,20,64]{0,2,1:T(8,128)S(1)} %bitcast.108), kind=kOutput, calls=%fused_computation.54 | convolution fusion | flops 252636160 | bytes 5591040 | tf_op jit(solution)/shard_map/thc,hcj->thj/dot_general | solution.py:85
  207.6 0.4 copy.64
  208.0 2.4 %fusion.17 = bf16[256,1280]{1,0:T(8,128)(2,1)} fusion(bf16[128,2,1280]{2,0,1:T(8,128)(2,1)} %all-to-all-done.4, f32[256,1280]{1,0:T(8,128)S(1)} %copy.64, f32[1280]{0:T(1024)S(1)} %dynamic_slice.35, f32[1280]{0:T(1024)S(1)} %dynamic_slice.34), kind=kLoop, calls=%fused_computation.24 | loop fusion | flops 2949120 | bytes 2631680 | tf_op jit(solution)/shard_map/convert_element_type | solution.py:93
  (60 shorter events, 1.2 us)
Async XLA Ops:
  6.5 123.8 %copy-start = (f32[40,64]{1,0:T(8,128)S(1)}, f32[40,64]{1,0:T(8,128)}, u32[]{:S(2)}) copy-start(f32[40,64]{1,0:T(8,128)} %param.17) | copy-start | bytes 30724
  6.5 5.6 %copy-start.7 = (bf16[128,2560]{1,0:T(8,128)(2,1)S(1)}, bf16[128,2560]{1,0:T(8,128)(2,1)}, u32[]{:S(2)}) copy-start(bf16[128,2560]{1,0:T(8,128)(2,1)} %param.13) | copy-start | bytes 1966084
  8.6 5.3 %all-to-all-start.2 = ((bf16[128,2,1280]{2,0,1:T(8,128)(2,1)}), bf16[128,2,1280]{2,0,1:T(8,128)(2,1)S(1)}, u32[]{:S(2)}, u32[]{:S(2)}) async-start(bf16[128,2,1280]{2,0,1:T(8,128)(2,1)} %bitcast.92), calls=%async_computation.2 | async-start | bytes 1310720 | tf_op jit(solution)/shard_map/all_to_all | solution.py:110
  13.9 8.1 %all-to-all-start.3 = ((bf16[128,2,1280]{0,2,1:T(8,128)(2,1)}), bf16[128,2,1280]{0,2,1:T(8,128)(2,1)S(1)}, u32[]{:S(2)}, u32[]{:S(2)}) async-start(bf16[128,2,1280]{0,2,1:T(8,128)(2,1)} %bitcast.10), calls=%async_computation.3 | async-start | bytes 1310720 | tf_op jit(solution)/shard_map/all_to_all | solution.py:108
  19.5 1.5 copy-start.8
  22.0 9.5 %all-to-all-start = ((bf16[128,2,1280]{0,2,1:T(8,128)(2,1)}), bf16[128,2,1280]{0,2,1:T(8,128)(2,1)S(1)}, u32[]{:S(2)}, u32[]{:S(2)}) async-start(bf16[128,2,1280]{0,2,1:T(8,128)(2,1)} %bitcast), calls=%async_computation | async-start | bytes 1310720 | tf_op jit(solution)/shard_map/all_to_all | solution.py:109
  25.6 155.6 %all-gather.3.cloned.1.call-start = ((), (), s32[]{:S(2)}) async-start(), calls=%async_computation.5 | async-start | bytes 11141120 | tf_op jit(solution)/shard_map/all_gather | solution.py:12
  31.5 0.8 copy-start.4
  40.7 3.4 %copy-start.3 = (bf16[256,20,64]{0,2,1:T(8,128)(2,1)}, bf16[256,20,64]{0,2,1:T(8,128)(2,1)S(1)}, u32[]{:S(2)}) copy-start(bf16[256,20,64]{0,2,1:T(8,128)(2,1)S(1)} %all_to_all.69) | copy-start | bytes 1966084
  46.3 7.8 %all-to-all-start.1 = ((bf16[128,2,1280]{0,2,1:T(8,128)(2,1)}), bf16[128,2,1280]{0,2,1:T(8,128)(2,1)S(1)}, u32[]{:S(2)}, u32[]{:S(2)}) async-start(bf16[128,2,1280]{0,2,1:T(8,128)(2,1)} %bitcast.3), calls=%async_computation.1 | async-start | bytes 1310720 | tf_op jit(solution)/shard_map/all_to_all | solution.py:107
  54.1 153.9 %all-to-all-start.4 = ((bf16[128,2,1280]{2,0,1:T(8,128)(2,1)}), bf16[128,2,1280]{2,0,1:T(8,128)(2,1)}, u32[]{:S(2)}, u32[]{:S(2)}) async-start(bf16[128,2,1280]{2,0,1:T(8,128)(2,1)} %bitcast.91), calls=%async_computation.4 | async-start | bytes 1310720 | tf_op jit(solution)/shard_map/all_to_all | solution.py:111
  63.2 1.1 copy-start.1
  81.2 3.2 %copy-start.9 = (f32[2560]{0:T(1024)S(1)}, f32[2560]{0:T(1024)}, u32[]{:S(2)}) copy-start(f32[2560]{0:T(1024)} %param.18) | copy-start | bytes 30724
  81.2 3.3 %copy-start.10 = (f32[2560]{0:T(1024)S(1)}, f32[2560]{0:T(1024)}, u32[]{:S(2)}) copy-start(f32[2560]{0:T(1024)} %param.19) | copy-start | bytes 30724
  130.4 3.2 %copy-start.5 = (f32[256,5,4,64]{0,3,2,1:T(8,128)S(1)}, f32[256,5,4,64]{0,3,2,1:T(8,128)}, u32[]{:S(2)}) copy-start(f32[256,5,4,64]{0,3,2,1:T(8,128)} %reshape.89) | copy-start | bytes 3932164
  130.4 3.2 %copy-start.6 = (f32[256,1280]{0,1:T(8,128)S(1)}, f32[256,1280]{0,1:T(8,128)}, u32[]{:S(2)}) copy-start(f32[256,1280]{0,1:T(8,128)} %copy.57) | copy-start | bytes 3932164
  181.1 23.3 %copy-start.2 = (f32[256,1280]{0,1:T(8,128)S(1)}, f32[256,1280]{0,1:T(8,128)}, u32[]{:S(2)}) copy-start(f32[256,1280]{0,1:T(8,128)} %copy.54) | copy-start | bytes 3932164
Sparse Core Ops, SparseCore 0:
  44.2 136.8 all-gather.2
where the time goes:
time: 219 us; the launch traced here: 217 us
  local copies, waits for them, and re-layouts  52.5 us (24%)
  blocking collectives  45.8 us (21%)
  other arithmetic  34.4 us (16%)
  matrix products  32.5 us (15%)
  waiting for transfers between devices  19.3 us (9%)
  starting transfers between devices  18.5 us (8%)
  between operations  13.7 us (6%)
    all_gather x1, blocking collectives, prefix_2(): pieces = jax.tree.map(lambda part: lax.all_gather(part, axis), value)  45.8 us
    select_n x15, other arithmetic, step(): jnp.where(position < mine, new, old)  22.7 us
    all_gather x1, waiting for transfers between devices, prefix_2(): pieces = jax.tree.map(lambda part: lax.all_gather(part, axis), value)  18.6 us
    dot_general x5, matrix products, group_output(): return jnp.einsum('hts,shj->thj', scores, values_group, precision=highest)  13.9 us
    dot_general x5, matrix products, group_output(): jnp.einsum('thc,shc->hts', receptance_group, keys_group, precision=highest)  10.6 us
    convert_element_type x3, local copies, waits for them, and re-layouts, block_shares(): query_vectors.astype(jnp.float32)  9.25 us
    transpose x2, local copies, waits for them, and re-layouts, group_heads(): array.reshape(length, groups, hosted_attenders // groups, channels)  8.76 us
    all_to_all x2, local copies, waits for them, and re-layouts, body(): lax.all_to_all(payload_vectors, 'head', split_axis=1, concat_axis=0, tile...  8.34 us
  transfers between devices with their start and end apart: 6, of which 2 were waited for; matrix products, arithmetic and copies ran while one was open for 47% of the time, Pallas kernels for 0%

commit v1 on v0

--- a/solution.py
+++ b/solution.py
@@ -5,6 +5,12 @@
 from jax.sharding import PartitionSpec as P
 
 CHANNEL_COUNT = 64
+
+
+def exchange_blocks(value, axis, split, join):
+    parts = jnp.split(value, lax.axis_size(axis), axis=split)
+    got = lax.all_to_all(jnp.stack(parts), axis, 0, 0)
+    return jnp.concatenate(got, axis=join)
 
 
 def prefix_2(value, axis, join, neutral):
@@ -106,7 +112,7 @@
     incoming_memory, address_block, payload_block, forget_multiplier, gate = (
         lax.all_to_all(query_vectors, "head", split_axis=1, concat_axis=0, tiled=True),
         lax.all_to_all(address_vectors, "head", split_axis=1, concat_axis=0, tiled=True),
-        lax.all_to_all(payload_vectors, "head", split_axis=1, concat_axis=0, tiled=True),
+        exchange_blocks(payload_vectors, "head", 1, 0),
         lax.all_to_all(forget_logarithms, "head", split_axis=1, concat_axis=0, tiled=True),
         lax.all_to_all(pre_sigmoid_filter, "head", split_axis=1, concat_axis=0, tiled=True),
     )

time: 219 us -> 212 us (0.968)
  local copies, waits for them, and re-layouts: 52.5 us -> 41 us
  waiting for transfers between devices: 19.3 us -> 24.2 us
    all_to_all x2 -> x1, local copies, waits for them, and re-layouts: 8.34 us -> 0.93 us  [exchange_blocks(): got = lax.all_to_all(jnp.stack(parts), axis, 0, 0)]
    all_gather x1, waiting for transfers between devices: 18.6 us -> 23.4 us  [prefix_2(): pieces = jax.tree.map(lambda part: lax.all_gather(part, axis), value)]
    transpose x2, local copies, waits for them, and re-layouts: 8.76 us -> 6.14 us  [group_heads(): array.reshape(length, groups, hosted_attenders // groups, channels)]
    unnamed x25 -> x22, local copies, waits for them, and re-layouts: 6.28 us -> 4.37 us
    transpose x3 -> x2, other arithmetic: 5.56 us -> 4.4 us  [group_heads(): array.reshape(length, groups, hosted_attenders // groups, channels)]
  transfers between devices with their start and end apart: 6 -> 6, of which waited for: 2 -> 2; matrix products, arithmetic and copies ran while one was open for 47% -> 46% of each run, Pallas kernels for 0% -> 0%
where the time goes in v1:
time: 212 us; the launch traced here: 210 us
  blocking collectives  45.5 us (21%)
  local copies, waits for them, and re-layouts  41 us (19%)
  other arithmetic  33.8 us (16%)
  matrix products  32.8 us (15%)
  waiting for transfers between devices  24.2 us (11%)
  starting transfers between devices  18.6 us (9%)
  between operations  13.7 us (6%)
    all_gather x1, blocking collectives, prefix_2(): pieces = jax.tree.map(lambda part: lax.all_gather(part, axis), value)  45.5 us
    all_gather x1, waiting for transfers between devices, prefix_2(): pieces = jax.tree.map(lambda part: lax.all_gather(part, axis), value)  23.4 us
    select_n x15, other arithmetic, step(): jnp.where(position < mine, new, old)  22.6 us
    dot_general x5, matrix products, group_output(): return jnp.einsum('hts,shj->thj', scores, values_group, precision=highest)  13.9 us
    dot_general x5, matrix products, group_output(): jnp.einsum('thc,shc->hts', receptance_group, keys_group, precision=highest)  10.6 us
    convert_element_type x3, local copies, waits for them, and re-layouts, block_shares(): query_vectors.astype(jnp.float32)  9.24 us
    convert_element_type x3, local copies, waits for them, and re-layouts, block_shares(): address_vectors.astype(jnp.float32)  7.94 us
    transpose x2, local copies, waits for them, and re-layouts, group_heads(): array.reshape(length, groups, hosted_attenders // groups, channels)  6.14 us
  transfers between devices with their start and end apart: 6, of which 2 were waited for; matrix products, arithmetic and copies ran while one was open for 46% of the time, Pallas kernels for 0%

profile of v1, /device:TPU:0, one launch (start us, length us, event | category | flops | bytes accessed | tf_op | source)
XLA Modules:
  0.0 210.1 jit_solution(12797497382640444796)
XLA Ops:
  6.5 2.0 copy.57
  8.6 3.5 %all-to-all-start.2 = ((bf16[128,2,1280]{2,0,1:T(8,128)(2,1)}), bf16[128,2,1280]{2,0,1:T(8,128)(2,1)S(1)}, u32[]{:S(2)}, u32[]{:S(2)}) async-start(bf16[128,2,1280]{2,0,1:T(8,128)(2,1)} %bitcast.93), calls=%async_computation.2 | async-start | bytes 1310720 | tf_op jit(solution)/shard_map/all_to_all | solution.py:116
  12.1 1.1 copy.40
  13.2 0.7 all-to-all-done.2
  13.9 3.5 %all-to-all-start.3 = ((bf16[128,2,1280]{0,2,1:T(8,128)(2,1)}), bf16[128,2,1280]{0,2,1:T(8,128)(2,1)S(1)}, u32[]{:S(2)}, u32[]{:S(2)}) async-start(bf16[128,2,1280]{0,2,1:T(8,128)(2,1)} %bitcast.10), calls=%async_computation.3 | async-start | bytes 1310720 | tf_op jit(solution)/shard_map/all_to_all | solution.py:114
  17.4 2.0 negate_exponential_fusion
  19.5 1.5 copy.46
  21.0 0.9 pad_maximum_fusion
  21.9 3.5 %all-to-all-start = ((bf16[2,128,1280]{2,1,0:T(8,128)(2,1)}), bf16[2,128,1280]{2,1,0:T(8,128)(2,1)S(1)}, u32[]{:S(2)}, u32[]{:S(2)}) async-start(bf16[2,128,1280]{2,1,0:T(8,128)(2,1)} %pad_maximum_fusion), calls=%async_computation | async-start | bytes 1310720 | tf_op jit(solution)/shard_map/all_to_all | solution.py:12
  25.6 4.8 %copy.41 = f32[2,128,1280]{1,0,2:T(2,128)S(1)} copy(f32[2,128,1280]{1,2,0:T(8,128)S(1)} %convert_bitcast_fusion) | data formatting | bytes 2621440 | tf_op jit(solution)/shard_map/convert_element_type | solution.py:53
  30.4 0.9 copy.45
  31.3 0.4 reshape.86
  31.7 1.0 reshape.92
  32.9 3.1 %fusion.22 = f32[20,64,64]{2,1,0:T(8,128)} fusion(bf16[256,20,64]{0,2,1:T(8,128)(2,1)S(1)} %reshape.86, f32[256,20,64]{0,2,1:T(8,128)S(1)} %reshape.92, f32[256,20,64]{0,2,1:T(8,128)} %bitcast.111, f32[20,64]{1,0:T(8,128)S(1)} %sub.22), kind=kOutput, calls=%fused_computation.32 | convolution fusion | flops 252313600 | bytes 3609600 | tf_op jit(solution)/shard_map/shc,shj->hcj/dot_general | solution.py:82
  36.0 2.2 %copy.36 = bf16[128,2560]{0,1:T(8,128)(2,1)} copy(bf16[128,2560]{1,0:T(8,128)(2,1)} %param.12) | data formatting | bytes 1310720 | tf_op args[0]
  38.2 3.5 %all-to-all-start.1 = ((bf16[128,2,1280]{0,2,1:T(8,128)(2,1)}), bf16[128,2,1280]{0,2,1:T(8,128)(2,1)S(1)}, u32[]{:S(2)}, u32[]{:S(2)}) async-start(bf16[128,2,1280]{0,2,1:T(8,128)(2,1)} %bitcast.3), calls=%async_computation.1 | async-start | bytes 1310720 | tf_op jit(solution)/shard_map/all_to_all | solution.py:113
  41.7 2.1 %reshape.90 = f32[256,5,4,64]{0,3,2,1:T(8,128)} reshape(f32[2,128,1280]{1,0,2:T(2,128)S(1)} %copy.41) | data formatting | bytes 2621440 | tf_op jit(solution)/shard_map/convert_element_type | solution.py:53
  43.8 2.0 copy.56
  45.8 4.5 %all-to-all-start.4 = ((bf16[128,2,1280]{2,0,1:T(8,128)(2,1)}), bf16[128,2,1280]{2,0,1:T(8,128)(2,1)}, u32[]{:S(2)}, u32[]{:S(2)}) async-start(bf16[128,2,1280]{2,0,1:T(8,128)(2,1)} %bitcast.92), calls=%async_computation.4 | async-start | bytes 1310720 | tf_op jit(solution)/shard_map/all_to_all | solution.py:117
  50.4 4.8 %copy.37 = f32[2,128,1280]{1,0,2:T(2,128)S(1)} copy(f32[2,128,1280]{1,2,0:T(8,128)S(1)} %convert_bitcast_fusion.1) | data formatting | bytes 2621440 | tf_op jit(solution)/shard_map/convert_element_type | solution.py:50
  55.2 1.1 copy-done.1
  56.2 2.1 %reshape.89 = f32[256,5,4,64]{0,3,2,1:T(8,128)} reshape(f32[2,128,1280]{1,0,2:T(2,128)S(1)} %copy.37) | data formatting | bytes 2621440 | tf_op jit(solution)/shard_map/convert_element_type | solution.py:50
  58.4 2.3 %reshape.91 = f32[256,20,64]{0,2,1:T(8,128)S(1)} reshape(f32[2,128,1280]{1,0,2:T(2,128)} %copy-done.1) | data formatting | bytes 2621440 | tf_op jit(solution)/shard_map/convert_element_type | solution.py:50
  60.7 2.8 %copy.39 = f32[256,1280]{0,1:T(8,128)} copy(f32[256,1280]{1,0:T(8,128)} %get-tuple-element.191) | data formatting | bytes 2621440 | tf_op jit(solution)/shard_map/exp | solution.py:59
  63.5 2.8 %copy.42 = f32[256,1280]{0,1:T(8,128)} copy(f32[256,1280]{1,0:T(8,128)} %get-tuple-element.190) | data formatting | bytes 2621440 | tf_op jit(solution)/shard_map/exp | solution.py:60
  66.3 3.0 %copy.35 = f32[2,128,1280]{1,0,2:T(2,128)} copy(bf16[2,128,1280]{2,1,0:T(8,128)(2,1)} %copy-done.3) | data formatting | bytes 1966080 | tf_op jit(solution)/shard_map/transpose | solution.py:32
  69.3 3.1 %reshape.94 = f32[256,5,4,64]{0,3,2,1:T(8,128)} reshape(f32[2,128,1280]{1,0,2:T(2,128)} %copy.35) | data formatting | bytes 2621440 | tf_op jit(solution)/shard_map/transpose | solution.py:32
  72.7 45.5 %all_gather.10 = f32[16,20,64]{2,1,0:T(8,128)S(1)} all-gather(f32[1,20,64]{2,1,0:T(8,128)S(1)} %exp.41), channel_id=1, replica_groups=mesh['seq'=16,'head'=2] {'seq'}, dimensions={0}, use_global_device_ids=true | all-gather | bytes 87040 | tf_op jit(solution)/shard_map/all_gather | solution.py:18
  118.2 3.2 %multiply_bitcast_fusion.1 = f32[5,256,4,64]{1,3,2,0:T(8,128)} fusion(f32[256,5,4,64]{0,3,2,1:T(8,128)} %reshape.89, f32[256,5,4,64]{0,3,2,1:T(8,128)} %bitcast.108), kind=kLoop, calls=%fused_computation.39 | loop fusion | flops 327680 | bytes 3932160 | tf_op jit(solution)/shard_map/transpose | solution.py:32
  121.4 1.2 multiply_bitcast_fusion
  122.6 24.7 %while.25 = (s32[]{:T(128)}, f32[5,256,4,64]{1,3,2,0:T(8,128)}, f32[5,256,4,64]{1,3,2,0:T(8,128)}, f32[5,256,4,64]{1,3,2,0:T(8,128)}, f32[5,256,4,64]{1,3,2,0:T(8,128)}, /*index=5*/s32[]{:T(128)}) while((s32[]{:T(128)}, f32[5,256,4,64]{1,3,2,0:T(8,128)}, f32[5,256,4,64]{1,3,2,0:T(8,128)}, f32[5,256,4,64]{1,3,2,0:T(8,128)}, ...), condition=%wide.region_1.2_spmd.clone, body=%wide.region_0.1_spmd.clone.sunk | while | flops 402980864 | bytes 3278917 | solution.py:71
  122.6 2.1 %convolution_select_fusion.2 = f32[4,256,256]{2,1,0:T(8,128)S(1)} fusion(pred[256,256]{1,0:T(8,128)(4,1)S(1)} %iota_compare_fusion.4, f32[5,256,4,64]{1,3,2,0:T(8,128)} %get-tuple-element.275, s32[]{:T(128)} %get-tuple-element.265, f32[5,256,4,64]{1,3,2,0:T(8,128)} %get-tuple-element.274), kind=kOutput, calls=%fused_computation.1.clone.1 | convolution fusion | flops 201588736 | bytes 1639424 | tf_op jit(solution)/shard_map/while/body/eval_jaxpr/thc,shc->hts/dot_general | solution.py:67
  124.8 2.8 %fusion.44 = f32[5,256,4,64]{1,3,2,0:T(8,128)} fusion(f32[5,256,4,64]{1,3,2,0:T(8,128)} %get-tuple-element.266, s32[]{:T(128)} %get-tuple-element.265, f32[4,256,256]{2,1,0:T(8,128)S(1)} %convolution_select_fusion.2, f32[5,256,4,64]{1,3,2,0:T(8,128)} %get-tuple-element.273), kind=kOutput, calls=%fused_computation.3.clone.1 | convolution fusion | flops 201326592 | bytes 1573888 | tf_op jit(solution)/shard_map/while/body/eval_jaxpr/hts,shj->thj/dot_general | solution.py:69
  127.6 2.1 %convolution_select_fusion.2 = f32[4,256,256]{2,1,0:T(8,128)S(1)} fusion(pred[256,256]{1,0:T(8,128)(4,1)S(1)} %iota_compare_fusion.4, f32[5,256,4,64]{1,3,2,0:T(8,128)} %get-tuple-element.275, s32[]{:T(128)} %get-tuple-element.265, f32[5,256,4,64]{1,3,2,0:T(8,128)} %get-tuple-element.274), kind=kOutput, calls=%fused_computation.1.clone.1 | convolution fusion | flops 201588736 | bytes 1639424 | tf_op jit(solution)/shard_map/while/body/eval_jaxpr/thc,shc->hts/dot_general | solution.py:67
  129.7 2.8 %fusion.44 = f32[5,256,4,64]{1,3,2,0:T(8,128)} fusion(f32[5,256,4,64]{1,3,2,0:T(8,128)} %get-tuple-element.266, s32[]{:T(128)} %get-tuple-element.265, f32[4,256,256]{2,1,0:T(8,128)S(1)} %convolution_select_fusion.2, f32[5,256,4,64]{1,3,2,0:T(8,128)} %get-tuple-element.273), kind=kOutput, calls=%fused_computation.3.clone.1 | convolution fusion | flops 201326592 | bytes 1573888 | tf_op jit(solution)/shard_map/while/body/eval_jaxpr/hts,shj->thj/dot_general | solution.py:69
  132.5 2.1 %convolution_select_fusion.2 = f32[4,256,256]{2,1,0:T(8,128)S(1)} fusion(pred[256,256]{1,0:T(8,128)(4,1)S(1)} %iota_compare_fusion.4, f32[5,256,4,64]{1,3,2,0:T(8,128)} %get-tuple-element.275, s32[]{:T(128)} %get-tuple-element.265, f32[5,256,4,64]{1,3,2,0:T(8,128)} %get-tuple-element.274), kind=kOutput, calls=%fused_computation.1.clone.1 | convolution fusion | flops 201588736 | bytes 1639424 | tf_op jit(solution)/shard_map/while/body/eval_jaxpr/thc,shc->hts/dot_general | solution.py:67
  134.6 2.8 %fusion.44 = f32[5,256,4,64]{1,3,2,0:T(8,128)} fusion(f32[5,256,4,64]{1,3,2,0:T(8,128)} %get-tuple-element.266, s32[]{:T(128)} %get-tuple-element.265, f32[4,256,256]{2,1,0:T(8,128)S(1)} %convolution_select_fusion.2, f32[5,256,4,64]{1,3,2,0:T(8,128)} %get-tuple-element.273), kind=kOutput, calls=%fused_computation.3.clone.1 | convolution fusion | flops 201326592 | bytes 1573888 | tf_op jit(solution)/shard_map/while/body/eval_jaxpr/hts,shj->thj/dot_general | solution.py:69
  137.4 2.1 %convolution_select_fusion.2 = f32[4,256,256]{2,1,0:T(8,128)S(1)} fusion(pred[256,256]{1,0:T(8,128)(4,1)S(1)} %iota_compare_fusion.4, f32[5,256,4,64]{1,3,2,0:T(8,128)} %get-tuple-element.275, s32[]{:T(128)} %get-tuple-element.265, f32[5,256,4,64]{1,3,2,0:T(8,128)} %get-tuple-element.274), kind=kOutput, calls=%fused_computation.1.clone.1 | convolution fusion | flops 201588736 | bytes 1639424 | tf_op jit(solution)/shard_map/while/body/eval_jaxpr/thc,shc->hts/dot_general | solution.py:67
  139.6 2.8 %fusion.44 = f32[5,256,4,64]{1,3,2,0:T(8,128)} fusion(f32[5,256,4,64]{1,3,2,0:T(8,128)} %get-tuple-element.266, s32[]{:T(128)} %get-tuple-element.265, f32[4,256,256]{2,1,0:T(8,128)S(1)} %convolution_select_fusion.2, f32[5,256,4,64]{1,3,2,0:T(8,128)} %get-tuple-element.273), kind=kOutput, calls=%fused_computation.3.clone.1 | convolution fusion | flops 201326592 | bytes 1573888 | tf_op jit(solution)/shard_map/while/body/eval_jaxpr/hts,shj->thj/dot_general | solution.py:69
  142.4 2.1 %convolution_select_fusion.2 = f32[4,256,256]{2,1,0:T(8,128)S(1)} fusion(pred[256,256]{1,0:T(8,128)(4,1)S(1)} %iota_compare_fusion.4, f32[5,256,4,64]{1,3,2,0:T(8,128)} %get-tuple-element.275, s32[]{:T(128)} %get-tuple-element.265, f32[5,256,4,64]{1,3,2,0:T(8,128)} %get-tuple-element.274), kind=kOutput, calls=%fused_computation.1.clone.1 | convolution fusion | flops 201588736 | bytes 1639424 | tf_op jit(solution)/shard_map/while/body/eval_jaxpr/thc,shc->hts/dot_general | solution.py:67
  144.5 2.8 %fusion.44 = f32[5,256,4,64]{1,3,2,0:T(8,128)} fusion(f32[5,256,4,64]{1,3,2,0:T(8,128)} %get-tuple-element.266, s32[]{:T(128)} %get-tuple-element.265, f32[4,256,256]{2,1,0:T(8,128)S(1)} %convolution_select_fusion.2, f32[5,256,4,64]{1,3,2,0:T(8,128)} %get-tuple-element.273), kind=kOutput, calls=%fused_computation.3.clone.1 | convolution fusion | flops 201326592 | bytes 1573888 | tf_op jit(solution)/shard_map/while/body/eval_jaxpr/hts,shj->thj/dot_general | solution.py:69
  147.3 2.9 %fusion.15 = f32[256,20,64]{0,2,1:T(8,128)} fusion(f32[256,20,64]{0,2,1:T(8,128)} %bitcast.15, bf16[256,20,64]{0,2,1:T(8,128)(2,1)} %copy-done.2, f32[256,20,64]{0,2,1:T(8,128)S(1)} %reshape.92, f32[256,20,64]{0,2,1:T(8,128)S(1)} %reshape.91, f32[20,64]{1,0:T(8,128)S(1)} %constant_dynamic-slice_fusion), kind=kOutput, calls=%fused_computation.20 | output fusion | flops 1643583 | bytes 5903360 | tf_op jit(solution)/shard_map/mul | solution.py:81
  150.2 23.4 %all-gather.3.cloned.1.call-done = f32[320,64,64]{2,1,0:T(8,128)} async-done(((f32[20,64,64]{2,1,0:T(8,128)}), f32[320,64,64]{2,1,0:T(8,128)}) %all-gather.3.cloned.1.call-update) | async-done | bytes 5242896 | tf_op jit(solution)/shard_map/all_gather | solution.py:18
  173.6 23.2 %while.26 = (s32[]{:T(128)}, f32[20,64,64]{2,1,0:T(8,128)S(1)}, s32[]{:T(128)}, f32[16,20,64]{2,1,0:T(8,128)S(1)}, f32[16,20,64,64]{3,2,1,0:T(8,128)}, /*index=5*/s32[]{:T(128)}, s32[]{:T(128)}) while((s32[]{:T(128)}, f32[20,64,64]{2,1,0:T(8,128)S(1)}, s32[]{:T(128)}, f32[16,20,64]{2,1,0:T(8,128)S(1)}, ...), condition=%wide.region_4.5_spmd.clone, body=%wide.region_3.4_spmd.clone.sunk | while | flops 327684 | bytes 998505 | solution.py:27
  173.6 1.5 fusion.45
  175.2 1.5 fusion.45
  176.7 1.5 fusion.45
  178.3 1.5 fusion.45
  179.8 1.5 fusion.45
  181.4 1.5 fusion.45
  182.9 1.5 fusion.45
  184.5 1.5 fusion.45
  186.0 1.5 fusion.45
  187.6 1.5 fusion.45
  189.2 1.5 fusion.45
  190.7 1.5 fusion.45
  192.3 1.5 fusion.45
  193.8 1.5 fusion.45
  195.4 1.5 fusion.45
  196.9 3.2 %fusion.29 = (f32[256,20]{0,1:T(8,128)S(1)}, f32[256,20,64]{0,2,1:T(8,128)S(1)}) fusion(f32[256,20,64]{0,2,1:T(8,128)} %fusion.15, f32[20,64,64]{2,1,0:T(8,128)S(1)} %get-tuple-element.132, f32[256,20,64]{0,2,1:T(8,128)S(1)} %reshape.91, f32[256,20,64]{0,2,1:T(8,128)} %bitcast.109), kind=kOutput, calls=%fused_computation.56 | convolution fusion | flops 252636160 | bytes 5591040 | tf_op jit(solution)/shard_map/thc,hcj->thj/dot_general | solution.py:91
  200.1 0.2 multiply_reduce_fusion
  200.3 0.2 subtract_multiply_fusion
  200.5 0.4 copy.49
  200.9 2.4 %fusion.17 = bf16[256,1280]{1,0:T(8,128)(2,1)} fusion(bf16[128,2,1280]{2,0,1:T(8,128)(2,1)} %all-to-all-done.4, f32[256,1280]{1,0:T(8,128)S(1)} %copy.49, f32[1280]{0:T(1024)S(1)} %dynamic_slice.35, f32[1280]{0:T(1024)S(1)} %dynamic_slice.34), kind=kLoop, calls=%fused_computation.24 | loop fusion | flops 2949120 | bytes 2631680 | tf_op jit(solution)/shard_map/convert_element_type | solution.py:99
  (58 shorter events, 0.9 us)
Async XLA Ops:
  6.5 111.6 %copy-start = (f32[40,64]{1,0:T(8,128)S(1)}, f32[40,64]{1,0:T(8,128)}, u32[]{:S(2)}) copy-start(f32[40,64]{1,0:T(8,128)} %param.17) | copy-start | bytes 30724
  6.5 5.6 %copy-start.6 = (bf16[128,2560]{1,0:T(8,128)(2,1)S(1)}, bf16[128,2560]{1,0:T(8,128)(2,1)}, u32[]{:S(2)}) copy-start(bf16[128,2560]{1,0:T(8,128)(2,1)} %param.13) | copy-start | bytes 1966084
  8.6 5.3 %all-to-all-start.2 = ((bf16[128,2,1280]{2,0,1:T(8,128)(2,1)}), bf16[128,2,1280]{2,0,1:T(8,128)(2,1)S(1)}, u32[]{:S(2)}, u32[]{:S(2)}) async-start(bf16[128,2,1280]{2,0,1:T(8,128)(2,1)} %bitcast.93), calls=%async_computation.2 | async-start | bytes 1310720 | tf_op jit(solution)/shard_map/all_to_all | solution.py:116
  13.9 8.0 %all-to-all-start.3 = ((bf16[128,2,1280]{0,2,1:T(8,128)(2,1)}), bf16[128,2,1280]{0,2,1:T(8,128)(2,1)S(1)}, u32[]{:S(2)}, u32[]{:S(2)}) async-start(bf16[128,2,1280]{0,2,1:T(8,128)(2,1)} %bitcast.10), calls=%async_computation.3 | async-start | bytes 1310720 | tf_op jit(solution)/shard_map/all_to_all | solution.py:114
  19.5 1.5 copy-start.7
  21.9 8.4 %all-to-all-start = ((bf16[2,128,1280]{2,1,0:T(8,128)(2,1)}), bf16[2,128,1280]{2,1,0:T(8,128)(2,1)S(1)}, u32[]{:S(2)}, u32[]{:S(2)}) async-start(bf16[2,128,1280]{2,1,0:T(8,128)(2,1)} %pad_maximum_fusion), calls=%async_computation | async-start | bytes 1310720 | tf_op jit(solution)/shard_map/all_to_all | solution.py:12
  25.4 148.2 %all-gather.3.cloned.1.call-start = ((), (), s32[]{:S(2)}) async-start(), calls=%async_computation.5 | async-start | bytes 11141120 | tf_op jit(solution)/shard_map/all_gather | solution.py:18
  30.4 1.0 copy-start.3
  31.7 1.1 copy-start.2
  38.2 7.6 %all-to-all-start.1 = ((bf16[128,2,1280]{0,2,1:T(8,128)(2,1)}), bf16[128,2,1280]{0,2,1:T(8,128)(2,1)S(1)}, u32[]{:S(2)}, u32[]{:S(2)}) async-start(bf16[128,2,1280]{0,2,1:T(8,128)(2,1)} %bitcast.3), calls=%async_computation.1 | async-start | bytes 1310720 | tf_op jit(solution)/shard_map/all_to_all | solution.py:113
  45.8 155.1 %all-to-all-start.4 = ((bf16[128,2,1280]{2,0,1:T(8,128)(2,1)}), bf16[128,2,1280]{2,0,1:T(8,128)(2,1)}, u32[]{:S(2)}, u32[]{:S(2)}) async-start(bf16[128,2,1280]{2,0,1:T(8,128)(2,1)} %bitcast.92), calls=%async_computation.4 | async-start | bytes 1310720 | tf_op jit(solution)/shard_map/all_to_all | solution.py:117
  55.1 1.1 copy-start.1
  69.3 3.2 %copy-start.8 = (f32[2560]{0:T(1024)S(1)}, f32[2560]{0:T(1024)}, u32[]{:S(2)}) copy-start(f32[2560]{0:T(1024)} %param.18) | copy-start | bytes 30724
  69.3 3.3 %copy-start.9 = (f32[2560]{0:T(1024)S(1)}, f32[2560]{0:T(1024)}, u32[]{:S(2)}) copy-start(f32[2560]{0:T(1024)} %param.19) | copy-start | bytes 30724
  118.2 3.2 %copy-start.4 = (f32[256,5,4,64]{0,3,2,1:T(8,128)S(1)}, f32[256,5,4,64]{0,3,2,1:T(8,128)}, u32[]{:S(2)}) copy-start(f32[256,5,4,64]{0,3,2,1:T(8,128)} %reshape.90) | copy-start | bytes 3932164
  118.2 3.2 %copy-start.5 = (f32[256,1280]{0,1:T(8,128)S(1)}, f32[256,1280]{0,1:T(8,128)}, u32[]{:S(2)}) copy-start(f32[256,1280]{0,1:T(8,128)} %copy.42) | copy-start | bytes 3932164
Sparse Core Ops, SparseCore 0:
  36.1 137.4 all-gather.2
